TPU v7x, 256 devices: a whole 4x4x8 slice. The times are simulated.
256 devices in a mesh: grid: 2 (over core), px: 16 (over y, x), py: 8 (over z).
Axes of the slice: x: 4, y: 4, z: 8, core: 2. Of those that a mesh axis runs over, the one named last changes fastest.
Arguments:
- residual: float32 [2, 128, 64, 5, 1024], P('grid', 'px', 'py'), may hold values from -3 to 3
- inverses: float32 [2, 128, 64, 25, 1024], P('grid', 'px', 'py'), may hold values from 0 to 1, as said below
- couplings: float32 [2, 128, 64, 4, 1024], P('grid', 'px', 'py'), may hold values from 0.22 to 0.735, as said below
- receptors: int32 [2, 16, 8, 512], P('grid', 'px', 'py'), may hold values from 0 to 65535, as said below
- owners: int32 [2, 16, 8, 512, 1], P('grid', 'px', 'py'), may hold values from 0 to 127; in each aligned block of 512 rows (0 to 511, 512 to 1023, ..., all dimensions but the last counted through in order) at most 8 rows name the same one
- donors: int32 [2, 16, 8, 512, 8], P('grid', 'px', 'py'), may hold values from 0 to 65535
- weights: float32 [2, 16, 8, 512, 8], P('grid', 'px', 'py'), may hold values from 0 to 1, as said below
Outputs:
- update: float32 [2, 128, 64, 5, 1024], P('grid', 'px', 'py')
Inputs may be any that keep to these rules, and one draw needn't show every extreme that they name: `receptors`: receptor indices of one device are distinct. `owners`: among the receptors of one device no owner appears more than 8 times, and in every draw some device names one owner exactly 8 times. `weights`: nonnegative; the 8 weights of a receptor sum to 1. `inverses`: all entries nonnegative; off-diagonal entries 0.02 to 0.07; each row of a block sums to 0.94 to 1. `couplings`: a + b and e + f of each cell lie in 0.88 to 0.98, and each coupling is a quarter to three quarters of its pair's sum.
All inputs are finite; a program needn't handle non-finite values.
Results may differ from a plain program's by a relative error of at most 0.0001.
Values sent between devices are 32-bit elements; how exact they have to be, the bound alone decides.
No kernel may reach another device: no remote copies, remote signals or barrier semaphores. Data moves between devices by JAX's collectives and lax.ppermute only.
A program may use at most 128 MiB of HBM per device.

v0:
```python
import jax
import jax.numpy as jnp
from jax import lax
from jax.sharding import PartitionSpec as P

KBLOCKS = 8


def from_behind(block, axis, distance):
    devices = range(lax.axis_size(axis))
    route = [(i - distance, i) for i in devices if i - distance in devices]
    return lax.ppermute(block, axis, route)


def swapped(array, axis, distance):
    return lax.ppermute(array, axis, [(i, i ^ 1 << distance) for i in range(lax.axis_size(axis))])


def grouped_exchange(array, axis, split_dim, concat_dim, work, item_dim, out_dim):
    items = jax.tree.leaves(array)[0].shape[item_dim]
    count = 2 if items % 2 == 0 else 1
    gathered = []
    for k in range(count):
        group = jax.tree.map(
            lambda a: lax.slice_in_dim(
                a, k * (items // count), (k + 1) * (items // count), axis=item_dim
            ),
            array,
        )
        gathered.append(
            work(
                lax.all_to_all(
                    group, axis, split_axis=split_dim, concat_axis=concat_dim, tiled=True
                )
            )
        )
    return jax.tree.map(lambda *parts: jnp.concatenate(parts, axis=out_dim), *gathered)


def apply_block(block, vector):
    shaped = block.reshape(block.shape[:-2] + (5, 5, block.shape[-1]))
    return jnp.sum(shaped * vector[..., None, :, :], axis=-2)


def sweep_forward(rhs_part, inverse_part, coupling_part, from_rows, from_columns):

    def row_step(upper_row, inputs):
        rhs_row, inv_row, coup_row, left_start = inputs
        left_value = left_start
        cell_list = []
        for column in range(rhs_row.shape[0]):
            left_value = apply_block(
                inv_row[column],
                rhs_row[column]
                + coup_row[column, 0][None] * upper_row[column]
                + coup_row[column, 1][None] * left_value,
            )
            cell_list.append(left_value)
        row_values = jnp.stack(cell_list)
        return (row_values, row_values)

    _, result = lax.scan(row_step, from_rows, (rhs_part, inverse_part, coupling_part, from_columns))
    return result


def sweep_backward(star_part, inverse_part, coupling_part, from_rows, from_columns):

    def row_step(lower_row, inputs):
        star_row, inv_row, coup_row, right_start = inputs
        right_value = right_start
        cell_list = [None] * star_row.shape[0]
        for column in reversed(range(star_row.shape[0])):
            right_value = star_row[column] + apply_block(
                inv_row[column],
                coup_row[column, 2][None] * lower_row[column]
                + coup_row[column, 3][None] * right_value,
            )
            cell_list[column] = right_value
        row_values = jnp.stack(cell_list)
        return (row_values, row_values)

    _, result = lax.scan(
        row_step, from_rows, (star_part, inverse_part, coupling_part, from_columns), reverse=True
    )
    return result


def local(residual, inverses, couplings, receptors, owners, donors, weights):
    rhs_local = residual[0]
    inverse_local = inverses[0]
    coupling_local = couplings[0]
    row_count, col_count, comp_count, pencil_length = rhs_local.shape
    block_count = KBLOCKS
    block_width = pencil_length // block_count
    place_rows = lax.axis_index("px")
    place_cols = lax.axis_index("py")
    count_rows = lax.axis_size("px")
    count_cols = lax.axis_size("py")
    sections = count_rows + count_cols - 1 + block_count - 1
    face_rows = jnp.zeros((col_count, comp_count, block_width), jnp.float32)
    face_cols = jnp.zeros((row_count, comp_count, block_width), jnp.float32)

    def slices(offset):
        return (
            lax.dynamic_slice_in_dim(inverse_local, offset, block_width, 3),
            lax.dynamic_slice_in_dim(coupling_local, offset, block_width, 3),
        )

    def forward_section(section_number, state_now):
        field_now, rows_now, cols_now = state_now
        from_rows = from_behind(rows_now, "px", 1)
        from_columns = from_behind(cols_now, "py", 1)
        block_index = section_number - place_rows - place_cols
        active = (block_index >= 0) & (block_index < block_count)
        offset = jnp.clip(block_index, 0, block_count - 1) * block_width

        def forward_compute(unused):
            inverse_part, coupling_part = slices(offset)
            rhs_part = lax.dynamic_slice_in_dim(rhs_local, offset, block_width, 3)
            result = sweep_forward(rhs_part, inverse_part, coupling_part, from_rows, from_columns)
            return (
                lax.dynamic_update_slice_in_dim(field_now, result, offset, 3),
                result[-1],
                result[:, -1],
            )

        def forward_keep(unused):
            return (field_now, rows_now, cols_now)

        return lax.cond(active, forward_compute, forward_keep, None)

    star_field = jnp.zeros_like(rhs_local)
    star_field, _, _ = lax.fori_loop(
        0, sections, forward_section, (star_field, face_rows, face_cols)
    )

    def backward_section(section_number, state_now):
        field_now, rows_now, cols_now = state_now
        from_rows = from_behind(rows_now, "px", -1)
        from_columns = from_behind(cols_now, "py", -1)
        block_index = section_number - (count_rows - 1 - place_rows) - (count_cols - 1 - place_cols)
        active = (block_index >= 0) & (block_index < block_count)
        offset = jnp.clip(block_index, 0, block_count - 1) * block_width

        def backward_compute(unused):
            inverse_part, coupling_part = slices(offset)
            star_part = lax.dynamic_slice_in_dim(star_field, offset, block_width, 3)
            result = sweep_backward(star_part, inverse_part, coupling_part, from_rows, from_columns)
            return (
                lax.dynamic_update_slice_in_dim(field_now, result, offset, 3),
                result[0],
                result[:, 0],
            )

        def backward_keep(unused):
            return (field_now, rows_now, cols_now)

        return lax.cond(active, backward_compute, backward_keep, None)

    swept_field = jnp.zeros_like(rhs_local)
    swept_field, _, _ = lax.fori_loop(
        0, sections, backward_section, (swept_field, face_rows, face_cols)
    )
    receptor_list = receptors[0, 0, 0]
    owner_list = owners[0, 0, 0, :, 0]
    donor_list = donors[0, 0, 0]
    weight_list = weights[0, 0, 0]
    receptor_count = receptor_list.shape[0]
    owner_count = count_rows * count_cols
    slot_count = max(2, 2 * receptor_count // owner_count)
    onehot = (owner_list[:, None] == jnp.arange(owner_count, dtype=jnp.int32)[None, :]).astype(
        jnp.int32
    )
    slot_rank = jnp.sum((jnp.cumsum(onehot, axis=0) - 1) * onehot, axis=1)
    slot_place = owner_list * slot_count + slot_rank
    request = (
        jnp.zeros((owner_count * slot_count, donor_list.shape[1]), jnp.int32)
        .at[slot_place]
        .set(donor_list)
    )
    request = request.reshape(owner_count, slot_count, donor_list.shape[1])
    flat_cells = swept_field.reshape(row_count * col_count, comp_count, pencil_length)

    def lookup(index_list):
        return flat_cells[index_list // pencil_length, :, index_list % pencil_length]

    moved_index = swapped(request, "grid", 0)
    values = grouped_exchange(moved_index, ("px", "py"), 0, 0, lookup, 1, 1)
    returned = lax.all_to_all(values, ("px", "py"), split_axis=0, concat_axis=0, tiled=True)
    returned = swapped(returned, "grid", 0)
    gathered = returned.reshape(owner_count * slot_count, donor_list.shape[1], comp_count)[
        slot_place
    ]
    fringe_values = jnp.sum(gathered * weight_list[..., None], axis=-2)
    refreshed = flat_cells.at[receptor_list // pencil_length, :, receptor_list % pencil_length].set(
        fringe_values
    )
    return refreshed.reshape(row_count, col_count, comp_count, pencil_length)[None]


def solution(mesh):
    placed = (
        P("grid", "px", "py", None, None),
        P("grid", "px", "py", None, None),
        P("grid", "px", "py", None, None),
        P("grid", "px", "py", None),
        P("grid", "px", "py", None, None),
        P("grid", "px", "py", None, None),
        P("grid", "px", "py", None, None),
    )
    return jax.shard_map(
        local,
        mesh=mesh,
        in_specs=placed,
        out_specs=P("grid", "px", "py", None, None),
        check_vma=False,
    )
```

profile of v0, /device:TPU:1, one launch (start us, length us, event | category | flops | bytes accessed | tf_op | source)
XLA Modules:
  0.0 1435.9 jit_solution(4124557084871150595)
XLA Ops:
  11.0 10.3 copy.93
  22.2 13.8 all-to-all-start
  37.6 380.9 %while.69 = (s32[]{:T(128)}, f32[8,8,5,1024]{3,2,1,0:T(8,128)}, f32[8,5,128]{2,1,0:T(8,128)S(1)}, f32[8,5,128]{2,1,0:T(8,128)S(1)}, s32[]{:T(128)}, /*index=5*/s...) while((s32[]{:T(128)}, f32[8,8,5,1024]{3,2,1,0:T(8,128)}, ...), condition=%wide.region_13.14_spmd, body=%wide.region_0.13_spmd.sunk | while | flops 66582 | bytes 3787170 | solution.py:133
  160.6 10.5 collective-permute-start.2
  177.7 12.2 collective-permute-start.3
  217.9 10.3 collective-permute-start.3
  231.2 9.8 collective-permute-start.3
  244.4 9.9 collective-permute-start.3
  257.2 10.2 collective-permute-start.3
  270.4 9.8 collective-permute-start.3
  296.4 11.5 collective-permute-start.3
  420.0 539.2 %while.70 = (s32[]{:T(128)}, f32[8,8,5,1024]{3,2,1,0:T(8,128)}, f32[8,5,128]{2,1,0:T(8,128)S(1)}, f32[8,5,128]{2,1,0:T(8,128)S(1)}, s32[]{:T(128)}, /*index=5*/s...) while((s32[]{:T(128)}, f32[8,8,5,1024]{3,2,1,0:T(8,128)}, ...), condition=%wide.region_27.28_spmd, body=%wide.region_14.27_spmd.sunk | while | flops 71063 | bytes 3927542 | solution.py:161
  624.0 195.6 %collective-permute-done = f32[8,5,128]{2,1,0:T(8,128)S(1)} collective-permute-done((f32[8,5,128]{2,1,0:T(8,128)S(1)}, f32[8,5,128]{2,1,0:T(8,128)S(1)}, u32[]{:S(2)}, u32[]{:S(2)}) %collective-permute-start) | collective-permute-done | bytes 20512 | tf_op jit(solution)/shard_map/while/body/eval_jaxpr/ppermute | solution.py:12
  819.6 9.7 conditional.5
  838.1 9.8 conditional.5
  912.7 9.7 conditional.5
  959.3 18.0 %copy.74 = f32[8,8,5,1024]{2,3,1,0:T(8,128)} copy(f32[8,8,5,1024]{3,2,1,0:T(8,128)} %get-tuple-element.674) | data formatting | bytes 2621440 | tf_op jit(solution)/shard_map/while | solution.py:161
  984.6 11.6 all-to-all-done.1
  997.1 171.2 %gather_fusion.1 = f32[4096,5]{1,0:T(8,128)S(1)} fusion(f32[64,5,1024]{1,2,0:T(8,128)} %bitcast.503, s32[4096]{0:T(1024)S(1)} %reshape.1313), kind=kCustom, calls=%fused_computation.1 | custom fusion | bytes 196608 | tf_op jit(solution)/shard_map/gather | solution.py:185
  1172.6 64.3 %gather_fusion = f32[4096,5]{1,0:T(8,128)S(1)} fusion(f32[64,5,1024]{1,2,0:T(8,128)} %bitcast.504, s32[4096]{0:T(1024)S(1)} %reshape.1307), kind=kCustom, calls=%fused_computation | custom fusion | bytes 196608 | tf_op jit(solution)/shard_map/gather | solution.py:185
  1245.0 43.6 %all_to_all.15 = f32[128,1,320]{2,1,0:T(1,128)S(1)} all-to-all(f32[128,1,320]{2,1,0:T(1,128)S(1)} %reshape.1367), channel_id=1, replica_groups=mesh['grid'=2,'px'=16,'py'=8] {'px','py'}, dimensions={0} | all-to-all | bytes 327680 | tf_op jit(solution)/shard_map/all_to_all | solution.py:189
  1291.9 60.9 %collective-permute-start.5 = (f32[128,8,8,5]{0,2,3,1:T(8,128)S(1)}, f32[128,8,8,5]{0,2,3,1:T(8,128)S(1)}, u32[]{:S(2)}, u32[]{:S(2)}) collective-permute-start(f32[128,8,8,5]{0,2,3,1:T(8,128)S(1)} %copy.80), channel_id=1, source_target_pairs={{0,128},{128,0},{1,129},{129,1},{2,130},{130,2},{3,131},{131,3},{4... | collective-permute-start | bytes 491528 | tf_op jit(solution)/shard_map/ppermute | solution.py:16
  1364.3 51.3 %scatter_fusion = f32[64,5,1024]{1,2,0:T(8,128)} fusion(f32[64,5,1024]{1,2,0:T(8,128)} %bitcast.505, s32[512]{0:T(512)S(1)} %bitcast.508, f32[512,5]{1,0:T(8,128)S(1)} %multiply_reduce_fusion.16), kind=kCustom, calls=%fused_computation.4 | custom fusion | bytes 34816 | tf_op jit(solution)/shard_map/scatter | solution.py:195
  1415.6 20.4 %copy.84 = f32[1,8,8,5,1024]{4,2,3,1,0:T(8,128)} copy(f32[1,8,8,5,1024]{3,4,2,1,0:T(8,128)} %bitcast.506) | data formatting | bytes 2621440 | tf_op jit(solution)/shard_map/broadcast_in_dim;reshape | solution.py:198
  (4688 shorter events, 855.0 us)
Async XLA Ops:
  5.5 15.8 %collective-permute-start.4 = (s32[128,8,8]{2,1,0:T(8,128)S(1)}, s32[128,8,8]{2,1,0:T(8,128)S(1)}, u32[]{:S(2)}, u32[]{:S(2)}) collective-permute-start(s32[128,8,8]{2,1,0:T(8,128)S(1)} %bitcast.514), channel_id=1, source_target_pairs={{0,128},{128,0},{1,129},{129,1},{2,130},{130,2},{3,131},{131,3},{4... | collective-permute-start | bytes 98312 | tf_op jit(solution)/shard_map/ppermute | solution.py:16
  22.2 955.1 %all-to-all-start = ((s32[128,4,8]{2,1,0:T(4,128)}), s32[128,4,8]{2,1,0:T(4,128)S(1)}, u32[]{:S(2)}, u32[]{:S(2)}) async-start(s32[128,4,8]{2,1,0:T(4,128)} %get-tuple-element.801), calls=%async_computation | async-start | bytes 524288 | tf_op jit(solution)/shard_map/all_to_all | solution.py:32
  160.6 14.2 collective-permute-start.2
  175.8 14.2 collective-permute-start.2
  177.7 13.2 collective-permute-start.3
  198.7 16.3 %collective-permute-start.2 = (f32[8,5,128]{2,1,0:T(8,128)S(1)}, f32[8,5,128]{2,1,0:T(8,128)S(1)}, u32[]{:S(2)}, u32[]{:S(2)}) collective-permute-start(f32[8,5,128]{2,1,0:T(8,128)S(1)} %get-tuple-element.1261), channel_id=1, source_target_pairs={{0,1},{1,2},{2,3},{3,4},{4,5},{5,6},{6,7},{8,9},{9,10},{10,11},{11... | collective-permute-start | bytes 61448 | tf_op jit(solution)/shard_map/while/body/eval_jaxpr/ppermute | solution.py:12
  216.0 12.3 collective-permute-start.2
  217.9 11.3 collective-permute-start.3
  229.2 11.8 collective-permute-start.2
  231.2 10.9 collective-permute-start.3
  242.0 12.3 collective-permute-start.2
  244.4 10.9 collective-permute-start.3
  255.3 12.2 collective-permute-start.2
  257.2 11.2 collective-permute-start.3
  268.5 11.7 collective-permute-start.2
  281.2 12.3 collective-permute-start.2
  294.4 13.5 collective-permute-start.2
  296.4 12.6 collective-permute-start.3
  317.6 12.3 collective-permute-start.2
  421.3 11.6 collective-permute-start.1
  621.4 198.2 %collective-permute-start = (f32[8,5,128]{2,1,0:T(8,128)S(1)}, f32[8,5,128]{2,1,0:T(8,128)S(1)}, u32[]{:S(2)}, u32[]{:S(2)}) collective-permute-start(f32[8,5,128]{2,1,0:T(8,128)S(1)} %get-tuple-element.1297), channel_id=1, source_target_pairs={{1,0},{2,1},{3,2},{4,3},{5,4},{6,5},{7,6},{9,8},{10,9},{11,10},{12... | collective-permute-start | bytes 61448 | tf_op jit(solution)/shard_map/while/body/eval_jaxpr/ppermute | solution.py:12
  622.7 196.9 %collective-permute-start.1 = (f32[8,5,128]{2,1,0:T(8,128)S(1)}, f32[8,5,128]{2,1,0:T(8,128)S(1)}, u32[]{:S(2)}, u32[]{:S(2)}) collective-permute-start(f32[8,5,128]{2,1,0:T(8,128)S(1)} %get-tuple-element.1296), channel_id=1, source_target_pairs={{8,0},{16,8},{24,16},{32,24},{40,32},{48,40},{56,48},{64,56},{72,6... | collective-permute-start | bytes 61448 | tf_op jit(solution)/shard_map/while/body/eval_jaxpr/ppermute | solution.py:12
  977.3 18.9 %all-to-all-start.1 = ((s32[128,4,8]{2,1,0:T(4,128)}), s32[128,4,8]{2,1,0:T(4,128)S(1)}, u32[]{:S(2)}, u32[]{:S(2)}) async-start(s32[128,4,8]{2,1,0:T(4,128)} %get-tuple-element.802), calls=%async_computation.1 | async-start | bytes 524288 | tf_op jit(solution)/shard_map/all_to_all | solution.py:32
  1291.9 62.0 %collective-permute-start.5 = (f32[128,8,8,5]{0,2,3,1:T(8,128)S(1)}, f32[128,8,8,5]{0,2,3,1:T(8,128)S(1)}, u32[]{:S(2)}, u32[]{:S(2)}) collective-permute-start(f32[128,8,8,5]{0,2,3,1:T(8,128)S(1)} %copy.80), channel_id=1, source_target_pairs={{0,128},{128,0},{1,129},{129,1},{2,130},{130,2},{3,131},{131,3},{4... | collective-permute-start | bytes 491528 | tf_op jit(solution)/shard_map/ppermute | solution.py:16
  (103 other events, 883.9 us)
where the time goes:
time: 1440 us
  starting transfers between devices  443 us (31%)
  local copies, waits for them, and re-layouts  442 us (31%)
  waiting for transfers between devices  425 us (30%)
  other arithmetic  46.8 us (3%)
  blocking collectives  43.6 us (3%)
  loops' own time  35 us (2%)
    ppermute x120, waiting for transfers between devices, from_behind(): return lax.ppermute(block, axis, route)  413 us
    ppermute x120, starting transfers between devices, from_behind(): return lax.ppermute(block, axis, route)  359 us
    gather x4, local copies, waits for them, and re-layouts, lookup(): flat_cells[index_list // pencil_length, :, index_list % pencil_length]  244 us
    ppermute x2, starting transfers between devices, swapped(): lax.ppermute(array, axis, [(i, i ^ 1 << distance) for i in range(lax.axis...  64.2 us
    scatter x1, local copies, waits for them, and re-layouts, local(): flat_cells.at[receptor_list // pencil_length, :, receptor_list % pencil_l...  51.3 us
    all_to_all x1, blocking collectives, local(): lax.all_to_all(values, ('px', 'py'), split_axis=0, concat_axis=0, tiled=T...  43.6 us

commit v1 on v0

v1 whole, which is shorter than its diff:
```python
import functools
import jax
import jax.numpy as jnp
from jax import lax
from jax.experimental import pallas as pl
from jax.experimental.pallas import tpu as pltpu
from jax.sharding import PartitionSpec as P

PERIOD = 8
LANES = 128
SUBS = 8
VM = pltpu.VMEM
F32 = jnp.float32


def vmem(value):
    return pltpu.with_memory_space_constraint(value, pltpu.VMEM)


def full(space):
    return pl.BlockSpec(memory_space=space)


def params(**kw):
    return pltpu.CompilerParams(vmem_limit_bytes=8 * 1024 * 1024, **kw)


def unpack_body(first, res, inv, cou, res_out, inv_out, cou_out, sem):
    del first
    for q in range(SUBS):
        lanes = pl.ds(q * LANES, LANES)
        for j in range(8):
            for n, (src, dst) in enumerate(((res, res_out), (inv, inv_out))):
                pltpu.make_async_copy(
                    src.at[:, :, j, lanes], dst.at[:, j, :, q, :], sem.at[n]
                ).start()
        pltpu.make_async_copy(cou.at[:, :, :, lanes], cou_out.at[:, :, :, q, :], sem.at[2]).start()
    for n, dst in enumerate((res_out, inv_out, cou_out)):
        pltpu.make_async_copy(dst, dst, sem.at[n]).wait()


def unpack(first, res, inv, cou):
    shapes = [(8, 8, w, SUBS, LANES) for w in (5, 25, 4)]
    hbm = lambda a: pltpu.with_memory_space_constraint(a, pltpu.HBM)
    out = pl.pallas_call(
        unpack_body,
        in_specs=[full(pl.ANY)] * 4,
        out_specs=[full(VM)] * 3,
        out_shape=[VM(shape, F32) for shape in shapes],
        scratch_shapes=[pltpu.SemaphoreType.DMA((3,))],
        compiler_params=params(),
        name="unpack",
    )(first, hbm(res), hbm(inv), hbm(cou))
    return [a.reshape((64,) + a.shape[2:]) for a in out]


def block_times(inv, p, vec):
    out = []
    for r in range(5):
        t = [inv[p, 5 * r + c] * vec[c] for c in range(5)]
        out.append(((t[0] + t[1]) + (t[2] + t[3])) + t[4])
    return out


def diagonal():
    return lax.axis_index("px") + lax.axis_index("py")


def forward_body(stage, rows_in, cols_in, res, inv, cou, star_in, rows_out, cols_out, star):
    @pl.when(diagonal() == stage)
    def _():
        rows_out[...] = rows_in[...]

        def row(i, carry):
            left = [cols_in[i, c] for c in range(5)]
            for j in range(8):
                p = i * 8 + j
                a, b = cou[p, 0], cou[p, 1]
                vec = [res[p, c] + a * rows_out[j, c] + b * left[c] for c in range(5)]
                left = block_times(inv, p, vec)
                for c in range(5):
                    rows_out[j, c] = left[c]
                    star[p, c] = left[c]
            for c in range(5):
                cols_out[i, c] = left[c]
            return carry

        lax.fori_loop(0, 8, row, 0)


def backward_body(stage, last, rows_in, cols_in, star, inv, cou, swept_in, rows_out, cols_out, swept):
    @pl.when(last - diagonal() == stage)
    def _():
        rows_out[...] = rows_in[...]

        def row(step, carry):
            i = 7 - step
            right = [cols_in[i, c] for c in range(5)]
            for j in range(7, -1, -1):
                p = i * 8 + j
                e, f = cou[p, 2], cou[p, 3]
                vec = [e * rows_out[j, c] + f * right[c] for c in range(5)]
                prod = block_times(inv, p, vec)
                right = [star[p, c] + prod[c] for c in range(5)]
                for c in range(5):
                    rows_out[j, c] = right[c]
                    swept[pl.ds(p * 64 + c, SUBS, stride=8), :] = right[c]
            for c in range(5):
                cols_out[i, c] = right[c]
            return carry

        lax.fori_loop(0, 8, row, 0)


def stage_call(body, name, faces, coeffs, state):
    face = VM(faces[0].shape, F32)
    count = len(faces) + len(coeffs)
    return pl.pallas_call(
        body,
        in_specs=[full(VM)] * (count + 1),
        out_specs=[full(VM)] * 3,
        out_shape=[face, face, VM(state.shape, F32)],
        input_output_aliases={count: 2},
        compiler_params=params(),
        name=name,
    )(*[vmem(a) for a in faces], *[vmem(a) for a in coeffs], vmem(state))


def routes(rows, cols, step, stage):
    px, py = [], []
    for i in range(rows):
        for j in range(cols):
            along = i + j if step > 0 else rows + cols - 2 - i - j
            if along % PERIOD == stage % PERIOD:
                if 0 <= i + step < rows:
                    px.append((i * cols + j, (i + step) * cols + j))
                if 0 <= j + step < cols:
                    py.append((i * cols + j, i * cols + j + step))
    return px, py


def pass_on(rows_face, cols_face, step, stage):
    px, py = routes(lax.axis_size("px"), lax.axis_size("py"), step, stage)
    return lax.ppermute(rows_face, ("px", "py"), px), lax.ppermute(cols_face, ("px", "py"), py)


def other_half():
    return (1 - lax.axis_index("grid")) * 128


def row_lane():
    return lax.broadcasted_iota(jnp.int32, (1, LANES), 1)


def request_body(owner, wanted, out, slots, count):
    out[...] = jnp.zeros_like(out)
    first = other_half()
    lane = row_lane()
    key = (lane & 63) >> 3

    def clear(o, carry):
        for n in range(8):
            count[o * 8 + n] = 0
        return carry

    lax.fori_loop(0, 16, clear, 0)

    def place(step, carry):
        for k in range(8):
            r = step * 8 + k
            o = owner[r]
            n = count[o]
            count[o] = n + 1
            slots[r] = o * 128 + n * 8
            pltpu.store(
                out.at[pl.ds(first + o, 1), :], wanted[pl.ds(r, 1), :], mask=key == n
            )
        return carry

    lax.fori_loop(0, wanted.shape[0] // 8, place, 0)


def make_request(owner, wanted):
    return pl.pallas_call(
        request_body,
        in_specs=[full(pltpu.SMEM), full(VM)],
        out_specs=[full(VM), full(pltpu.SMEM)],
        out_shape=[
            jax.ShapeDtypeStruct((256, LANES), F32),
            jax.ShapeDtypeStruct(owner.shape, jnp.int32),
        ],
        scratch_shapes=[pltpu.SMEM((128,), jnp.int32)],
        compiler_params=params(),
        name="request",
    )(owner, wanted)


def picks_body(late, asked, picks_in, picks):
    del picks_in
    first = other_half()
    lane = lax.broadcasted_iota(jnp.int32, (64, LANES), 1)

    @pl.when((diagonal() >= 12) == late)
    def _():
        def group(t, carry):
            rows = asked[pl.ds(pl.multiple_of(first + t * 8, 8), 8), :]
            turned = rows.T
            cell = turned[:64].astype(jnp.int32) & 127
            weight = turned[64:]
            for k in range(8):
                at = pl.multiple_of((t * 8 + k) * 64, 64)
                picks[pl.ds(at, 64), :] = jnp.where(
                    lane == cell[:, k : k + 1], weight[:, k : k + 1], 0.0
                )
            return carry

        lax.fori_loop(0, 16, group, 0)


def make_picks(late, asked, picks):
    return pl.pallas_call(
        functools.partial(picks_body, late),
        in_specs=[full(VM)] * 2,
        out_specs=full(VM),
        out_shape=VM(picks.shape, F32),
        input_output_aliases={1: 0},
        compiler_params=params(),
        name="picks",
    )(asked, vmem(picks))


def serve_body(index, picks, swept, out):
    out[...] = jnp.zeros_like(out)
    first = other_half()

    def pair(t, carry):
        sums = []
        for n in range(16):
            total = None
            for d in range(8):
                row = pl.multiple_of(index[t * 2 + n // 8, n % 8 * 8 + d], 8)
                pick = picks[pl.ds(t * 128 + n * 8 + d, 1), :]
                part = swept[pl.ds(row, 8), :] * pick
                total = part if total is None else total + part
            sums.append(total)
        flat = jnp.sum(jnp.concatenate(sums, axis=0).T, axis=0, keepdims=True)
        out[pl.ds(first + t * 2, 1), :] = flat
        out[pl.ds(first + t * 2 + 1, 1), :] = pltpu.roll(flat, 64, axis=1)
        return carry

    lax.fori_loop(0, 64, pair, 0)


def serve(index, picks, swept):
    return pl.pallas_call(
        serve_body,
        in_specs=[full(pltpu.SMEM), full(VM), full(VM)],
        out_specs=full(VM),
        out_shape=jax.ShapeDtypeStruct((256, LANES), F32),
        compiler_params=params(),
        name="serve",
    )(index, vmem(picks), vmem(swept))


def finish_body(receptors, slots, values, swept_in, out, swept, sem):
    lane = lax.broadcasted_iota(jnp.int32, (SUBS, LANES), 1)
    sub = lax.broadcasted_iota(jnp.int32, (SUBS, LANES), 0)

    def put(step, carry):
        for k in range(8):
            cell = receptors[step * 8 + k]
            at = slots[step * 8 + k]
            row = pl.multiple_of((cell >> 7) * 8, 8)
            new = jnp.full((SUBS, LANES), values[at], F32)
            for c in range(1, 5):
                new = jnp.where(sub == c, values[at + c], new)
            pltpu.store(swept.at[pl.ds(row, 8), :], new, mask=lane == (cell & 127))
        return carry

    lax.fori_loop(0, receptors.shape[0] // 8, put, 0)
    view = swept.reshape(8, 8, SUBS, 8, LANES)
    for q in range(SUBS):
        for j in range(8):
            pltpu.make_async_copy(
                view.at[:, j, q, pl.ds(0, 5), :],
                out.at[:, :, j, pl.ds(q * LANES, LANES)],
                sem.at[0],
            ).start()
    pltpu.make_async_copy(out, out, sem.at[0]).wait()


def finish(receptors, slots, values, swept):
    out, _ = pl.pallas_call(
        finish_body,
        in_specs=[full(pltpu.SMEM)] * 3 + [full(VM)],
        out_specs=[full(pl.ANY), full(VM)],
        out_shape=[pltpu.HBM((8, 5, 8, 1024), F32), VM(swept.shape, F32)],
        input_output_aliases={3: 1},
        scratch_shapes=[pltpu.SemaphoreType.DMA((1,))],
        compiler_params=params(),
        name="finish",
    )(receptors, slots, values, vmem(swept))
    return out


def exchange(rows):
    return lax.all_to_all(rows, ("grid", "px", "py"), split_axis=0, concat_axis=0, tiled=True)


def local(residual, inverses, couplings, receptors, owners, donors, weights):
    rows = lax.axis_size("px")
    cols = lax.axis_size("py")
    last = rows + cols - 2

    cells = jnp.tile(donors[0, 0, 0].astype(F32), (1, 8))
    wanted = jnp.concatenate([cells, jnp.tile(weights[0, 0, 0], (1, 8))], axis=1)
    request, slots = make_request(owners[0, 0, 0, :, 0], wanted)
    asked = exchange(request)
    asked_row = lax.dynamic_slice(asked, (other_half(), 0), (128, 64)).astype(jnp.int32) >> 7 << 3
    picks = jnp.zeros((8192, LANES), F32)

    by_row = lambda a: a[0].transpose(0, 2, 1, 3)
    res, inv, cou = unpack(asked_row, by_row(residual), by_row(inverses), couplings[0])

    faces = (jnp.zeros((8, 5, SUBS, LANES), F32),) * 2
    star = jnp.zeros((64, 5, SUBS, LANES), F32)
    for stage in range(last + 1):
        if stage:
            faces = pass_on(*faces, 1, stage - 1)
        *faces, star = stage_call(
            functools.partial(forward_body, stage), "forward", faces, (res, inv, cou), star
        )
        if stage in (2, 20):
            picks = make_picks(stage == 2, asked, picks)
    faces = (jnp.zeros((8, 5, SUBS, LANES), F32),) * 2
    swept = jnp.zeros((64 * SUBS * 8, LANES), F32)
    for stage in range(last + 1):
        if stage:
            faces = pass_on(*faces, -1, stage - 1)
        *faces, swept = stage_call(
            functools.partial(backward_body, stage, last), "backward", faces, (star, inv, cou), swept
        )

    answers = exchange(serve(asked_row, picks, swept)).reshape(256 * LANES)
    answers = lax.dynamic_slice(answers, (other_half() * LANES,), (128 * LANES,))
    out = finish(receptors[0, 0, 0], slots, answers, swept)
    return out.transpose(0, 2, 1, 3)[None]


def solution(mesh):
    placed = (
        P("grid", "px", "py", None, None),
        P("grid", "px", "py", None, None),
        P("grid", "px", "py", None, None),
        P("grid", "px", "py", None),
        P("grid", "px", "py", None, None),
        P("grid", "px", "py", None, None),
        P("grid", "px", "py", None, None),
    )
    return jax.shard_map(
        local,
        mesh=mesh,
        in_specs=placed,
        out_specs=P("grid", "px", "py", None, None),
        check_vma=False,
    )
```

time: 1440 us -> 392 us (0.27)
  local copies, waits for them, and re-layouts: 442 us -> 1.46 us
  starting transfers between devices: 443 us -> 141 us
  waiting for transfers between devices: 425 us -> 204 us
  other arithmetic: 46.8 us -> 0.89 us
  blocking collectives: 43.6 us -> 0 us
  Pallas kernels: 0 us -> 41.3 us
  loops' own time: 35 us -> 0 us
    ppermute x122 -> x88, starting transfers between devices: 423 us -> 79.5 us  [the longest x44 45.3 us: pass_on(): lax.ppermute(rows_face, ('px', 'py'), px)]
    gather x5 -> x0, local copies, waits for them, and re-layouts: 247 us -> none  [the longest x4 244 us: lookup(): flat_cells[index_list // pencil_length, :, index_list % pencil_length]]
    ppermute x122 -> x88, waiting for transfers between devices: 413 us -> 178 us  [the longest x44 173 us: pass_on(): lax.ppermute(rows_face, ('px', 'py'), px)]
    scatter x2 -> x0, local copies, waits for them, and re-layouts: 53.1 us -> none  [the longest x1 51.3 us: local(): flat_cells.at[receptor_list // pencil_length, :, receptor_list % pencil_l...]
    dynamic_slice x48 -> x1, local copies, waits for them, and re-layouts: 51.6 us -> 0.01 us  [local(): lax.dynamic_slice(answers, (other_half() * LANES,), (128 * LANES,))]
    all_to_all x1 -> x0, blocking collectives: 43.6 us -> none  [local(): lax.all_to_all(values, ('px', 'py'), split_axis=0, concat_axis=0, tiled=T...]
    all_to_all x2, starting transfers between devices: 20.1 us -> 61.8 us  [exchange(): lax.all_to_all(rows, ('grid', 'px', 'py'), split_axis=0, concat_axis=0, t...]
    pallas_call x0 -> x52, Pallas kernels: none -> 41.3 us  [the longest x1 18.4 us: serve(): pl.pallas_call(serve_body, in_specs=[full(pltpu.SMEM), full(VM), full(VM)...]
where the time goes in v1:
time: 392 us; the launch traced here: 391 us
  waiting for transfers between devices  204 us (52%)
  starting transfers between devices  141 us (36%)
  Pallas kernels  41.3 us (11%)
    ppermute x44, waiting for transfers between devices, pass_on(): lax.ppermute(rows_face, ('px', 'py'), px)  173 us
    all_to_all x2, starting transfers between devices, exchange(): lax.all_to_all(rows, ('grid', 'px', 'py'), split_axis=0, concat_axis=0, t...  61.8 us
    ppermute x44, starting transfers between devices, pass_on(): lax.ppermute(rows_face, ('px', 'py'), px)  45.3 us
    ppermute x44, starting transfers between devices, pass_on(): lax.ppermute(cols_face, ('px', 'py'), py)  34.2 us
    all_to_all x2, waiting for transfers between devices, exchange(): lax.all_to_all(rows, ('grid', 'px', 'py'), split_axis=0, concat_axis=0, t...  25.7 us
    pallas_call x1, Pallas kernels, serve(): pl.pallas_call(serve_body, in_specs=[full(pltpu.SMEM), full(VM), full(VM)...  18.4 us
  transfers between devices with their start and end apart: 90, of which 11 were waited for; matrix products, arithmetic and copies ran while one was open for 0% of the time, Pallas kernels for 1%

profile of v1, /device:TPU:1, one launch (start us, length us, event | category | flops | bytes accessed | tf_op | source)
XLA Modules:
  0.0 390.5 jit_solution(7169469892462118572)
XLA Ops:
  1.9 4.1 %request.1 = (f32[256,128]{1,0:T(8,128)}, s32[512]{0:T(512)S(1)}) custom-call(s32[512]{0:T(512)S(1)} %bitcast.152, f32[512,128]{1,0:T(8,128)S(1)} %pad_maximum_fusion.wanted), custom_call_target="tpu_custom_call" | custom-call | tf_op jit(solution)/shard_map/request/pallas_call | solution.py:184
  5.9 15.7 %all-to-all-start = ((f32[256,1,128]{2,1,0:T(1,128)}), f32[256,1,128]{2,1,0:T(1,128)S(1)}, u32[]{:S(2)}, u32[]{:S(2)}) async-start(f32[256,1,128]{2,1,0:T(1,128)} %bitcast.7), calls=%async_computation | async-start | bytes 262144 | tf_op jit(solution)/shard_map/all_to_all | solution.py:307
  21.6 12.8 %all-to-all-done = f32[256,1,128]{2,1,0:T(1,128)S(1)} async-done(((f32[256,1,128]{2,1,0:T(1,128)}), f32[256,1,128]{2,1,0:T(1,128)S(1)}, u32[]{:S(2)}, u32[]{:S(2)}) %all-to-all-start) | async-done | bytes 131104 | tf_op jit(solution)/shard_map/all_to_all | solution.py:307
  34.4 4.8 %unpack.1 = (f32[8,8,5,8,128]{4,3,2,1,0:T(8,128)S(1)}, f32[8,8,25,8,128]{4,3,2,1,0:T(8,128)S(1)}, f32[8,8,4,8,128]{4,3,2,1,0:T(8,128)S(1)}) custom-call(s32[128,64]{1,0:T(8,128)S(1)} %shift-left_bitcast_fusion.first.index, f32[8,5,8,1024]{3,2,1,0:T(8,128)} %bitcast.155, f32[8,25,8,1024]{3,2,1,0:T(8,128)} %bitcast.154, f32[8,8,4,1024]{3,2,1,0:T(4,128)} %bitcast.156), custom_call_target="tpu_custom_call" | custom-call | tf_op jit(solution)/shard_map/unpack/pallas_call | solution.py:45
  40.0 1.4 collective-permute-start
  41.5 1.3 collective-permute-start.1
  42.8 1.5 collective-permute-done.rows_in
  44.3 1.3 collective-permute-done.1.cols_in
  55.5 6.9 %collective-permute-start.16 = (f32[8,5,8,128]{3,2,1,0:T(8,128)S(1)}, f32[8,5,8,128]{3,2,1,0:T(8,128)S(1)}, u32[]{:S(2)}, u32[]{:S(2)}) collective-permute-start(f32[8,5,8,128]{3,2,1,0:T(8,128)S(1)} %get-tuple-element.174), channel_id=1, source_target_pairs={{0,8},{15,23},{22,30},{29,37},{36,44},{43,51},{50,58},{57,65},{64,... | collective-permute-start | bytes 491528 | tf_op jit(solution)/shard_map/ppermute | solution.py:144
  62.4 2.0 collective-permute-start.17
  64.6 2.0 collective-permute-done.17.cols_in
  76.5 7.6 %collective-permute-start.32 = (f32[8,5,8,128]{3,2,1,0:T(8,128)S(1)}, f32[8,5,8,128]{3,2,1,0:T(8,128)S(1)}, u32[]{:S(2)}, u32[]{:S(2)}) collective-permute-start(f32[8,5,8,128]{3,2,1,0:T(8,128)S(1)} %get-tuple-element.198), channel_id=1, source_target_pairs={{0,8},{15,23},{22,30},{29,37},{36,44},{43,51},{50,58},{57,65},{64,... | collective-permute-start | bytes 491528 | tf_op jit(solution)/shard_map/ppermute | solution.py:144
  84.0 1.4 collective-permute-start.33
  86.3 1.4 collective-permute-done.33.cols_in
  102.6 1.3 collective-permute-start.54
  105.2 55.2 %collective-permute-done.54.rows_in = f32[8,5,8,128]{3,2,1,0:T(8,128)S(1)} collective-permute-done((f32[8,5,8,128]{3,2,1,0:T(8,128)S(1)}, f32[8,5,8,128]{3,2,1,0:T(8,128)S(1)}, u32[]{:S(2)}, u32[]{:S(2)}) %collective-permute-start.54) | collective-permute-done | bytes 163872 | tf_op jit(solution)/shard_map/ppermute | solution.py:144
  173.0 55.0 %collective-permute-done.70.rows_in = f32[8,5,8,128]{3,2,1,0:T(8,128)S(1)} collective-permute-done((f32[8,5,8,128]{3,2,1,0:T(8,128)S(1)}, f32[8,5,8,128]{3,2,1,0:T(8,128)S(1)}, u32[]{:S(2)}, u32[]{:S(2)}) %collective-permute-start.70) | collective-permute-done | bytes 163872 | tf_op jit(solution)/shard_map/ppermute | solution.py:144
  240.8 5.2 %picks.3 = f32[8192,128]{1,0:T(8,128)S(1)} custom-call(f32[256,128]{1,0:T(8,128)S(1)} %bitcast.151, f32[8192,128]{1,0:T(8,128)S(1)} %picks.2.picks_in), custom_call_target="tpu_custom_call", output_to_operand_aliasing={{}: (1, {})} | custom-call | tf_op jit(solution)/shard_map/picks/pallas_call | solution.py:221
  246.0 60.2 %collective-permute-done.86.rows_in = f32[8,5,8,128]{3,2,1,0:T(8,128)S(1)} collective-permute-done((f32[8,5,8,128]{3,2,1,0:T(8,128)S(1)}, f32[8,5,8,128]{3,2,1,0:T(8,128)S(1)}, u32[]{:S(2)}, u32[]{:S(2)}) %collective-permute-start.86) | collective-permute-done | bytes 163872 | tf_op jit(solution)/shard_map/ppermute | solution.py:144
  306.2 1.4 backward.45
  307.6 18.4 %serve.1 = f32[256,128]{1,0:T(8,128)} custom-call(s32[128,64]{1,0:T(8,128)S(1)} %shift-left_bitcast_fusion.first.index, f32[8192,128]{1,0:T(8,128)S(1)} %picks.3, f32[4096,128]{1,0:T(8,128)S(1)} %get-tuple-element.283.swept.swept_in), custom_call_target="tpu_custom_call" | custom-call | tf_op jit(solution)/shard_map/serve/pallas_call | solution.py:255
  326.0 46.2 %all-to-all-start.1 = ((f32[256,1,128]{2,1,0:T(1,128)}), f32[256,1,128]{2,1,0:T(1,128)S(1)}, u32[]{:S(2)}, u32[]{:S(2)}) async-start(f32[256,1,128]{2,1,0:T(1,128)} %bitcast.20), calls=%async_computation.1 | async-start | bytes 262144 | tf_op jit(solution)/shard_map/all_to_all | solution.py:307
  372.2 12.9 %all-to-all-done.1 = f32[256,1,128]{2,1,0:T(1,128)S(1)} async-done(((f32[256,1,128]{2,1,0:T(1,128)}), f32[256,1,128]{2,1,0:T(1,128)S(1)}, u32[]{:S(2)}, u32[]{:S(2)}) %all-to-all-start.1) | async-done | bytes 131104 | tf_op jit(solution)/shard_map/all_to_all | solution.py:307
  385.1 5.2 %finish.1 = (f32[8,5,8,1024]{3,2,1,0:T(8,128)}, f32[4096,128]{1,0:T(8,128)S(1)}) custom-call(s32[512]{0:T(512)S(1)} %bitcast.153, s32[512]{0:T(512)S(1)} %get-tuple-element.145.slots, f32[16384]{0:T(1024)S(1)} %dynamic_slice.7.values, f32[4096,128]{1,0:T(8,128)S(1)} %get-tuple-element.283.swept.swept_in), custom_call_target="tpu_custom_call", output_to_operand_aliasing={{1}: (3, {})} | custom-call | tf_op jit(solution)/shard_map/finish/pallas_call | solution.py:293
  (226 shorter events, 63.4 us)
Async XLA Ops:
  5.9 28.5 %all-to-all-start = ((f32[256,1,128]{2,1,0:T(1,128)}), f32[256,1,128]{2,1,0:T(1,128)S(1)}, u32[]{:S(2)}, u32[]{:S(2)}) async-start(f32[256,1,128]{2,1,0:T(1,128)} %bitcast.7), calls=%async_computation | async-start | bytes 262144 | tf_op jit(solution)/shard_map/all_to_all | solution.py:307
  40.0 4.3 %collective-permute-start = (f32[8,5,8,128]{3,2,1,0:T(8,128)S(1)}, f32[8,5,8,128]{3,2,1,0:T(8,128)S(1)}, u32[]{:S(2)}, u32[]{:S(2)}) collective-permute-start(f32[8,5,8,128]{3,2,1,0:T(8,128)S(1)} %get-tuple-element.150), channel_id=1, source_target_pairs={{0,8},{15,23},{22,30},{29,37},{36,44},{43,51},{50,58},{57,65},{64,... | collective-permute-start | bytes 491528 | tf_op jit(solution)/shard_map/ppermute | solution.py:144
  41.5 4.1 %collective-permute-start.1 = (f32[8,5,8,128]{3,2,1,0:T(8,128)S(1)}, f32[8,5,8,128]{3,2,1,0:T(8,128)S(1)}, u32[]{:S(2)}, u32[]{:S(2)}) collective-permute-start(f32[8,5,8,128]{3,2,1,0:T(8,128)S(1)} %get-tuple-element.151), channel_id=1, source_target_pairs={{0,1},{22,23},{29,30},{36,37},{43,44},{50,51},{57,58},{64,65},{86,... | collective-permute-start | bytes 491528 | tf_op jit(solution)/shard_map/ppermute | solution.py:144
  48.4 1.4 collective-permute-start.6
  51.2 1.4 collective-permute-start.10
  54.0 1.4 collective-permute-start.14
  55.5 9.2 %collective-permute-start.16 = (f32[8,5,8,128]{3,2,1,0:T(8,128)S(1)}, f32[8,5,8,128]{3,2,1,0:T(8,128)S(1)}, u32[]{:S(2)}, u32[]{:S(2)}) collective-permute-start(f32[8,5,8,128]{3,2,1,0:T(8,128)S(1)} %get-tuple-element.174), channel_id=1, source_target_pairs={{0,8},{15,23},{22,30},{29,37},{36,44},{43,51},{50,58},{57,65},{64,... | collective-permute-start | bytes 491528 | tf_op jit(solution)/shard_map/ppermute | solution.py:144
  62.4 4.2 %collective-permute-start.17 = (f32[8,5,8,128]{3,2,1,0:T(8,128)S(1)}, f32[8,5,8,128]{3,2,1,0:T(8,128)S(1)}, u32[]{:S(2)}, u32[]{:S(2)}) collective-permute-start(f32[8,5,8,128]{3,2,1,0:T(8,128)S(1)} %get-tuple-element.175), channel_id=1, source_target_pairs={{0,1},{22,23},{29,30},{36,37},{43,44},{50,51},{57,58},{64,65},{86,... | collective-permute-start | bytes 491528 | tf_op jit(solution)/shard_map/ppermute | solution.py:144
  69.4 1.4 collective-permute-start.22
  72.2 1.4 collective-permute-start.26
  75.1 1.4 collective-permute-start.30
  76.5 9.8 %collective-permute-start.32 = (f32[8,5,8,128]{3,2,1,0:T(8,128)S(1)}, f32[8,5,8,128]{3,2,1,0:T(8,128)S(1)}, u32[]{:S(2)}, u32[]{:S(2)}) collective-permute-start(f32[8,5,8,128]{3,2,1,0:T(8,128)S(1)} %get-tuple-element.198), channel_id=1, source_target_pairs={{0,8},{15,23},{22,30},{29,37},{36,44},{43,51},{50,58},{57,65},{64,... | collective-permute-start | bytes 491528 | tf_op jit(solution)/shard_map/ppermute | solution.py:144
  84.0 3.6 collective-permute-start.33
  96.9 1.4 collective-permute-start.46
  102.6 57.8 %collective-permute-start.54 = (f32[8,5,8,128]{3,2,1,0:T(8,128)S(1)}, f32[8,5,8,128]{3,2,1,0:T(8,128)S(1)}, u32[]{:S(2)}, u32[]{:S(2)}) collective-permute-start(f32[8,5,8,128]{3,2,1,0:T(8,128)S(1)} %get-tuple-element.232), channel_id=1, source_target_pairs={{8,0},{23,15},{30,22},{37,29},{44,36},{51,43},{58,50},{65,57},{72,... | collective-permute-start | bytes 491528 | tf_op jit(solution)/shard_map/ppermute | solution.py:144
  103.9 56.5 %collective-permute-start.55 = (f32[8,5,8,128]{3,2,1,0:T(8,128)S(1)}, f32[8,5,8,128]{3,2,1,0:T(8,128)S(1)}, u32[]{:S(2)}, u32[]{:S(2)}) collective-permute-start(f32[8,5,8,128]{3,2,1,0:T(8,128)S(1)} %get-tuple-element.233), channel_id=1, source_target_pairs={{1,0},{23,22},{30,29},{37,36},{44,43},{51,50},{58,57},{65,64},{87,... | collective-permute-start | bytes 491528 | tf_op jit(solution)/shard_map/ppermute | solution.py:144
  163.2 1.4 collective-permute-start.60
  167.4 1.5 collective-permute-start.66
  170.4 57.6 %collective-permute-start.70 = (f32[8,5,8,128]{3,2,1,0:T(8,128)S(1)}, f32[8,5,8,128]{3,2,1,0:T(8,128)S(1)}, u32[]{:S(2)}, u32[]{:S(2)}) collective-permute-start(f32[8,5,8,128]{3,2,1,0:T(8,128)S(1)} %get-tuple-element.256), channel_id=1, source_target_pairs={{8,0},{23,15},{30,22},{37,29},{44,36},{51,43},{58,50},{65,57},{72,... | collective-permute-start | bytes 491528 | tf_op jit(solution)/shard_map/ppermute | solution.py:144
  171.7 56.3 %collective-permute-start.71 = (f32[8,5,8,128]{3,2,1,0:T(8,128)S(1)}, f32[8,5,8,128]{3,2,1,0:T(8,128)S(1)}, u32[]{:S(2)}, u32[]{:S(2)}) collective-permute-start(f32[8,5,8,128]{3,2,1,0:T(8,128)S(1)} %get-tuple-element.257), channel_id=1, source_target_pairs={{1,0},{23,22},{30,29},{37,36},{44,43},{51,50},{58,57},{65,64},{87,... | collective-permute-start | bytes 491528 | tf_op jit(solution)/shard_map/ppermute | solution.py:144
  235.1 1.4 collective-permute-start.82
  237.9 68.3 %collective-permute-start.86 = (f32[8,5,8,128]{3,2,1,0:T(8,128)S(1)}, f32[8,5,8,128]{3,2,1,0:T(8,128)S(1)}, u32[]{:S(2)}, u32[]{:S(2)}) collective-permute-start(f32[8,5,8,128]{3,2,1,0:T(8,128)S(1)} %get-tuple-element.280), channel_id=1, source_target_pairs={{8,0},{23,15},{30,22},{37,29},{44,36},{51,43},{58,50},{65,57},{72,... | collective-permute-start | bytes 491528 | tf_op jit(solution)/shard_map/ppermute | solution.py:144
  239.2 67.0 %collective-permute-start.87 = (f32[8,5,8,128]{3,2,1,0:T(8,128)S(1)}, f32[8,5,8,128]{3,2,1,0:T(8,128)S(1)}, u32[]{:S(2)}, u32[]{:S(2)}) collective-permute-start(f32[8,5,8,128]{3,2,1,0:T(8,128)S(1)} %get-tuple-element.281), channel_id=1, source_target_pairs={{1,0},{23,22},{30,29},{37,36},{44,43},{51,50},{58,57},{65,64},{87,... | collective-permute-start | bytes 491528 | tf_op jit(solution)/shard_map/ppermute | solution.py:144
  326.0 59.1 %all-to-all-start.1 = ((f32[256,1,128]{2,1,0:T(1,128)}), f32[256,1,128]{2,1,0:T(1,128)S(1)}, u32[]{:S(2)}, u32[]{:S(2)}) async-start(f32[256,1,128]{2,1,0:T(1,128)} %bitcast.20), calls=%async_computation.1 | async-start | bytes 262144 | tf_op jit(solution)/shard_map/all_to_all | solution.py:307
  (69 other events, 143.6 us)

commit v2 on v1

v2 whole, which is shorter than its diff:
```python
import functools
import jax
import jax.numpy as jnp
from jax import lax
from jax.experimental import pallas as pl
from jax.experimental.pallas import tpu as pltpu
from jax.sharding import PartitionSpec as P

PERIOD = 8
PARTS = 2
LAG = 2
LANES = 128
SUBS = 8
VM = pltpu.VMEM
F32 = jnp.float32


def vmem(value):
    return pltpu.with_memory_space_constraint(value, pltpu.VMEM)


def full(space):
    return pl.BlockSpec(memory_space=space)


def params(**kw):
    return pltpu.CompilerParams(vmem_limit_bytes=8 * 1024 * 1024, **kw)


def prepare_body(
    owner, donors, weights, res, inv, cou, out, slots, res_out, inv_out, cou_out, wanted, count, sem
):
    for q in range(SUBS):
        lanes = pl.ds(q * LANES, LANES)
        for j in range(8):
            for n, (src, dst) in enumerate(((res, res_out), (inv, inv_out))):
                pltpu.make_async_copy(
                    src.at[:, :, j, lanes], dst.at[:, j, :, q, :], sem.at[n]
                ).start()
        pltpu.make_async_copy(cou.at[:, :, :, lanes], cou_out.at[:, :, :, q, :], sem.at[2]).start()

    out[...] = jnp.zeros_like(out)
    wanted[...] = jnp.concatenate([donors[...].astype(F32)] * 8 + [weights[...]] * 8, axis=0).T
    first = other_half()
    key = (row_lane() & 63) >> 3

    def clear(step, carry):
        for n in range(8):
            count[step * 8 + n] = 0
        return carry

    lax.fori_loop(0, 16, clear, 0)

    def place(step, carry):
        for k in range(8):
            r = step * 8 + k
            o = owner[r]
            n = count[o]
            count[o] = n + 1
            slots[r] = o * 128 + n * 8
            pltpu.store(
                out.at[pl.ds(first + o, 1), :], wanted[pl.ds(r, 1), :], mask=key == n
            )
        return carry

    lax.fori_loop(0, wanted.shape[0] // 8, place, 0)
    for n, dst in enumerate((res_out, inv_out, cou_out)):
        pltpu.make_async_copy(dst, dst, sem.at[n]).wait()


def prepare(owner, donors, weights, res, inv, cou):
    shapes = [(8, 8, w, SUBS, LANES) for w in (5, 25, 4)]
    hbm = lambda a: pltpu.with_memory_space_constraint(a, pltpu.HBM)
    request, slots, *rest = pl.pallas_call(
        prepare_body,
        in_specs=[full(pltpu.SMEM), full(VM), full(VM)] + [full(pl.ANY)] * 3,
        out_specs=[full(VM), full(pltpu.SMEM)] + [full(VM)] * 3,
        out_shape=[
            VM((256, LANES), F32),
            jax.ShapeDtypeStruct(owner.shape, jnp.int32),
        ]
        + [VM(shape, F32) for shape in shapes],
        scratch_shapes=[
            pltpu.VMEM((512, LANES), F32),
            pltpu.SMEM((128,), jnp.int32),
            pltpu.SemaphoreType.DMA((3,)),
        ],
        compiler_params=params(),
        name="prepare",
    )(owner, donors, weights, hbm(res), hbm(inv), hbm(cou))
    return request, slots, [a.reshape((64,) + a.shape[2:]) for a in rest]


def block_times(inv, p, part, vec):
    out = []
    for r in range(5):
        t = [inv[p, 5 * r + c, part, :] * vec[c] for c in range(5)]
        out.append(((t[0] + t[1]) + (t[2] + t[3])) + t[4])
    return out


def diagonal():
    return lax.axis_index("px") + lax.axis_index("py")


def parts_due(stage, arrival):
    def call(work):
        for n in range(PARTS):
            size = SUBS // PARTS

            @pl.when(arrival + LAG * n == stage)
            def _():
                work(n * size, slice(n * size, (n + 1) * size))

    return call


def forward_body(stage, rows_in, cols_in, res, inv, cou, star_in, rows_out, cols_out, star):
    @parts_due(stage, diagonal())
    def _(start, part):
        rows_out[...] = rows_in[...]

        def row(i, carry):
            left = [cols_in[i, c] for c in range(5)]
            for j in range(8):
                p = i * 8 + j
                a, b = cou[p, 0, part, :], cou[p, 1, part, :]
                vec = [res[p, c, part, :] + a * rows_out[j, c] + b * left[c] for c in range(5)]
                left = block_times(inv, p, part, vec)
                for c in range(5):
                    rows_out[j, c] = left[c]
                    star[p, c, part, :] = left[c]
            for c in range(5):
                cols_out[i, c] = left[c]
            return carry

        lax.fori_loop(0, 8, row, 0)


def backward_body(stage, last, rows_in, cols_in, star, inv, cou, swept_in, rows_out, cols_out, swept):
    @parts_due(stage, last - diagonal())
    def _(start, part):
        rows_out[...] = rows_in[...]

        def row(step, carry):
            i = 7 - step
            right = [cols_in[i, c] for c in range(5)]
            for j in range(7, -1, -1):
                p = i * 8 + j
                e, f = cou[p, 2, part, :], cou[p, 3, part, :]
                vec = [e * rows_out[j, c] + f * right[c] for c in range(5)]
                prod = block_times(inv, p, part, vec)
                right = [star[p, c, part, :] + prod[c] for c in range(5)]
                for c in range(5):
                    rows_out[j, c] = right[c]
                    swept[pl.ds(p * 64 + start * 8 + c, SUBS // PARTS, stride=8), :] = right[c]
            for c in range(5):
                cols_out[i, c] = right[c]
            return carry

        lax.fori_loop(0, 8, row, 0)


def stage_call(body, name, faces, coeffs, state, after=()):
    face = VM(faces[0].shape, F32)
    count = len(faces) + len(coeffs)

    def run(*refs):
        body(*refs[: count + 1], *refs[count + 1 + len(after) :])

    return pl.pallas_call(
        run,
        in_specs=[full(VM)] * (count + 1) + [full(pl.ANY)] * len(after),
        out_specs=[full(VM)] * 3,
        out_shape=[face, face, VM(state.shape, F32)],
        input_output_aliases={count: 2},
        compiler_params=params(),
        name=name,
    )(*[vmem(a) for a in faces], *[vmem(a) for a in coeffs], vmem(state), *after)


def routes(rows, cols, step, stage):
    px, py = [], []
    for i in range(rows):
        for j in range(cols):
            along = i + j if step > 0 else rows + cols - 2 - i - j
            if any((stage - LAG * n - along) % PERIOD == 0 for n in range(PARTS)):
                if 0 <= i + step < rows:
                    px.append((i * cols + j, (i + step) * cols + j))
                if 0 <= j + step < cols:
                    py.append((i * cols + j, i * cols + j + step))
    return px, py


def pass_on(rows_face, cols_face, step, stage):
    px, py = routes(lax.axis_size("px"), lax.axis_size("py"), step, stage)
    return lax.ppermute(rows_face, ("px", "py"), px), lax.ppermute(cols_face, ("px", "py"), py)


def other_half():
    return (1 - lax.axis_index("grid")) * 128


def row_lane():
    return lax.broadcasted_iota(jnp.int32, (1, LANES), 1)


def fill_picks(asked, picks):
    first = other_half()
    lane = lax.broadcasted_iota(jnp.int32, (64, LANES), 1)

    def group(t, carry):
        turned = asked[pl.ds(pl.multiple_of(first + t * 8, 8), 8), :].T
        cell = turned[:64].astype(jnp.int32) & 127
        weight = turned[64:]
        for k in range(8):
            at = pl.multiple_of((t * 8 + k) * 64, 64)
            picks[pl.ds(at, 64), :] = jnp.where(
                lane == cell[:, k : k + 1], weight[:, k : k + 1], 0.0
            )
        return carry

    lax.fori_loop(0, 16, group, 0)


def late_body(asked, picks):
    @pl.when(diagonal() >= 12)
    def _():
        fill_picks(asked, picks)


def early_body(asked, picks_in, picks, rows):
    del picks_in
    first = pl.multiple_of(other_half(), 128)
    rows[...] = asked[pl.ds(first, 128), :].astype(jnp.int32) >> 7 << 3

    @pl.when(diagonal() < 12)
    def _():
        fill_picks(asked, picks)


def late_picks(asked):
    return pl.pallas_call(
        late_body,
        in_specs=[full(VM)],
        out_specs=full(VM),
        out_shape=VM((8192, LANES), F32),
        compiler_params=params(),
        name="late",
    )(vmem(asked))


def early_picks(asked, picks):
    return pl.pallas_call(
        early_body,
        in_specs=[full(VM)] * 2,
        out_specs=[full(VM)] * 2,
        out_shape=[VM(picks.shape, F32), VM((128, LANES), jnp.int32)],
        input_output_aliases={1: 0},
        compiler_params=params(),
        name="early",
    )(vmem(asked), vmem(picks))


def serve_body(index, picks, swept, out, sums):
    out[...] = jnp.zeros_like(out)
    first = other_half()

    def write(t):
        flat = jnp.sum(sums[...].T, axis=0, keepdims=True)
        out[pl.ds(first + t * 2, 1), :] = flat
        out[pl.ds(first + t * 2 + 1, 1), :] = pltpu.roll(flat, 64, axis=1)

    def pair(t, carry):
        write(jnp.maximum(t - 1, 0))
        for n in range(16):
            total = None
            for d in range(8):
                row = pl.multiple_of(index[t * 2 + n // 8, n % 8 * 8 + d], 8)
                pick = picks[pl.ds(t * 128 + n * 8 + d, 1), :]
                part = swept[pl.ds(row, 8), :] * pick
                total = part if total is None else total + part
            sums[pl.ds(n * 8, 8), :] = total
        return carry

    sums[...] = jnp.zeros_like(sums)
    lax.fori_loop(0, 64, pair, 0)
    write(63)


def serve(index, picks, swept):
    return pl.pallas_call(
        serve_body,
        in_specs=[full(pltpu.SMEM), full(VM), full(VM)],
        out_specs=full(VM),
        out_shape=jax.ShapeDtypeStruct((256, LANES), F32),
        scratch_shapes=[pltpu.VMEM((LANES, LANES), F32)],
        compiler_params=params(),
        name="serve",
    )(index, vmem(picks), vmem(swept))


def finish_body(receptors, slots, values, swept_in, out, swept, sem):
    lane = lax.broadcasted_iota(jnp.int32, (SUBS, LANES), 1)
    sub = lax.broadcasted_iota(jnp.int32, (SUBS, LANES), 0)

    def put(step, carry):
        for k in range(8):
            cell = receptors[step * 8 + k]
            at = slots[step * 8 + k]
            row = pl.multiple_of((cell >> 7) * 8, 8)
            new = jnp.full((SUBS, LANES), values[at], F32)
            for c in range(1, 5):
                new = jnp.where(sub == c, values[at + c], new)
            pltpu.store(swept.at[pl.ds(row, 8), :], new, mask=lane == (cell & 127))
        return carry

    lax.fori_loop(0, receptors.shape[0] // 8, put, 0)
    view = swept.reshape(8, 8, SUBS, 8, LANES)
    for q in range(SUBS):
        for j in range(8):
            pltpu.make_async_copy(
                view.at[:, j, q, pl.ds(0, 5), :],
                out.at[:, :, j, pl.ds(q * LANES, LANES)],
                sem.at[0],
            ).start()
    pltpu.make_async_copy(out, out, sem.at[0]).wait()


def finish(receptors, slots, values, swept):
    out, _ = pl.pallas_call(
        finish_body,
        in_specs=[full(pltpu.SMEM)] * 3 + [full(VM)],
        out_specs=[full(pl.ANY), full(VM)],
        out_shape=[pltpu.HBM((8, 5, 8, 1024), F32), VM(swept.shape, F32)],
        input_output_aliases={3: 1},
        scratch_shapes=[pltpu.SemaphoreType.DMA((1,))],
        compiler_params=params(),
        name="finish",
    )(receptors, slots, values, vmem(swept))
    return out


def exchange(rows):
    return lax.all_to_all(rows, ("grid", "px", "py"), split_axis=0, concat_axis=0, tiled=True)


def local(residual, inverses, couplings, receptors, owners, donors, weights):
    rows = lax.axis_size("px")
    cols = lax.axis_size("py")
    last = rows + cols - 2

    by_row = lambda a: a[0].transpose(0, 2, 1, 3)
    request, slots, (res, inv, cou) = prepare(
        owners[0, 0, 0, :, 0],
        donors[0, 0, 0].T,
        weights[0, 0, 0].T,
        by_row(residual),
        by_row(inverses),
        couplings[0],
    )
    asked = exchange(request)

    faces = (jnp.zeros((8, 5, SUBS // PARTS, LANES), F32),) * 2
    star = jnp.zeros((64, 5, SUBS, LANES), F32)
    for stage in range(last + 1 + LAG * (PARTS - 1)):
        if stage:
            faces = pass_on(*faces, 1, stage - 1)
        *faces, star = stage_call(
            functools.partial(forward_body, stage),
            "forward",
            faces,
            (res, inv, cou),
            star,
            (picks,) if stage == 5 else (),
        )
        if stage == 4:
            picks = late_picks(asked)
        if stage == 20:
            picks, asked_row = early_picks(asked, picks)
    faces = (jnp.zeros((8, 5, SUBS // PARTS, LANES), F32),) * 2
    swept = jnp.zeros((64 * SUBS * 8, LANES), F32)
    for stage in range(last + 1 + LAG * (PARTS - 1)):
        if stage:
            faces = pass_on(*faces, -1, stage - 1)
        *faces, swept = stage_call(
            functools.partial(backward_body, stage, last),
            "backward",
            faces,
            (star, inv, cou),
            swept,
            () if stage else (asked_row,),
        )

    answers = exchange(serve(asked_row, picks, swept)).reshape(256 * LANES)
    answers = lax.dynamic_slice(answers, (other_half() * LANES,), (128 * LANES,))
    out = finish(receptors[0, 0, 0], slots, answers, swept)
    return out.transpose(0, 2, 1, 3)[None]


def solution(mesh):
    placed = (
        P("grid", "px", "py", None, None),
        P("grid", "px", "py", None, None),
        P("grid", "px", "py", None, None),
        P("grid", "px", "py", None),
        P("grid", "px", "py", None, None),
        P("grid", "px", "py", None, None),
        P("grid", "px", "py", None, None),
    )
    return jax.shard_map(
        local,
        mesh=mesh,
        in_specs=placed,
        out_specs=P("grid", "px", "py", None, None),
        check_vma=False,
    )
```

time: 392 us -> 371 us (0.946)
  waiting for transfers between devices: 204 us -> 149 us
  starting transfers between devices: 141 us -> 171 us
  local copies, waits for them, and re-layouts: 1.46 us -> 12.3 us
  Pallas kernels: 41.3 us -> 35.4 us
    ppermute x44 -> x48, waiting for transfers between devices: 173 us -> 128 us  [pass_on(): lax.ppermute(rows_face, ('px', 'py'), px)]
    ppermute x44 -> x48, starting transfers between devices: 45.3 us -> 67.2 us  [pass_on(): lax.ppermute(rows_face, ('px', 'py'), px)]
    all_to_all x2, waiting for transfers between devices: 25.7 us -> 12.9 us  [exchange(): lax.all_to_all(rows, ('grid', 'px', 'py'), split_axis=0, concat_axis=0, t...]
    unnamed x6 -> x28, local copies, waits for them, and re-layouts: 0.68 us -> 12 us
    ppermute x44 -> x48, starting transfers between devices: 34.2 us -> 39.6 us  [pass_on(): lax.ppermute(cols_face, ('px', 'py'), py)]
    pallas_call x1, Pallas kernels: 18.4 us -> 13.8 us  [serve(): pl.pallas_call(serve_body, in_specs=[full(pltpu.SMEM), full(VM), full(VM)...]
    ppermute x44 -> x48, waiting for transfers between devices: 4.82 us -> 7.92 us  [pass_on(): lax.ppermute(cols_face, ('px', 'py'), py)]
    pallas_call x50 -> x53, Pallas kernels: 17.7 us -> 16.3 us  [the longest x1 6 us: prepare(): pl.pallas_call(prepare_body, in_specs=[full(pltpu.SMEM), full(VM), full(V...]
  transfers between devices with their start and end apart: 90 -> 98, of which waited for: 11 -> 19; matrix products, arithmetic and copies ran while one was open for 0% -> 0% of each run, Pallas kernels for 1% -> 2%
where the time goes in v2:
time: 371 us; the launch traced here: 370 us
  starting transfers between devices  171 us (46%)
  waiting for transfers between devices  149 us (40%)
  Pallas kernels  35.4 us (10%)
  local copies, waits for them, and re-layouts  12.3 us (3%)
    ppermute x48, waiting for transfers between devices, pass_on(): lax.ppermute(rows_face, ('px', 'py'), px)  128 us
    ppermute x48, starting transfers between devices, pass_on(): lax.ppermute(rows_face, ('px', 'py'), px)  67.2 us
    all_to_all x2, starting transfers between devices, exchange(): lax.all_to_all(rows, ('grid', 'px', 'py'), split_axis=0, concat_axis=0, t...  64.6 us
    ppermute x48, starting transfers between devices, pass_on(): lax.ppermute(cols_face, ('px', 'py'), py)  39.6 us
    pallas_call x1, Pallas kernels, serve(): pl.pallas_call(serve_body, in_specs=[full(pltpu.SMEM), full(VM), full(VM)...  13.8 us
    all_to_all x2, waiting for transfers between devices, exchange(): lax.all_to_all(rows, ('grid', 'px', 'py'), split_axis=0, concat_axis=0, t...  12.9 us
    unnamed x28, local copies, waits for them, and re-layouts  12 us
    ppermute x48, waiting for transfers between devices, pass_on(): lax.ppermute(cols_face, ('px', 'py'), py)  7.92 us
  transfers between devices with their start and end apart: 98, of which 19 were waited for; matrix products, arithmetic and copies ran while one was open for 0% of the time, Pallas kernels for 2%

profile of v2, /device:TPU:1, one launch (start us, length us, event | category | flops | bytes accessed | tf_op | source)
XLA Modules:
  0.0 369.6 jit_solution(1372857654711048086)
XLA Ops:
  2.1 6.0 %prepare.1 = (f32[256,128]{1,0:T(8,128)}, s32[512]{0:T(512)S(1)}, f32[8,8,5,8,128]{4,3,2,1,0:T(8,128)S(1)}, f32[8,8,25,8,128]{4,3,2,1,0:T(8,128)S(1)}, f32[8,8,4,8,128]{4,3,2,1,0:T(8,128)S(1)}) custom-call(s32[512]{0:T(512)S(1)} %bitcast.160, s32[8,512]{1,0:T(8,128)S(1)} %bitcast.158, f32[8,512]{1,0:T(8,128)S(1)} %bitcast.159, f32[8,5,8,1024]{3,2,1,0:T(8,128)} %bitcast.163, ...), custom_call_target="tpu_custom_call" | custom-call | tf_op jit(solution)/shard_map/prepare/pallas_call | solution.py:74
  9.0 3.3 collective-permute-start
  16.3 18.8 %all-to-all-start = ((f32[256,1,128]{2,1,0:T(1,128)}), f32[256,1,128]{2,1,0:T(1,128)S(1)}, u32[]{:S(2)}, u32[]{:S(2)}) async-start(f32[256,1,128]{2,1,0:T(1,128)} %bitcast.12), calls=%async_computation | async-start | bytes 262144 | tf_op jit(solution)/shard_map/all_to_all | solution.py:345
  35.2 2.9 copy-done.1
  38.0 1.3 copy-done.6
  40.0 2.6 collective-permute-start.4
  49.4 2.9 copy-done.2
  56.5 8.0 %collective-permute-start.16 = (f32[8,5,4,128]{3,2,1,0:T(4,128)S(1)}, f32[8,5,4,128]{3,2,1,0:T(4,128)S(1)}, u32[]{:S(2)}, u32[]{:S(2)}) collective-permute-start(f32[8,5,4,128]{3,2,1,0:T(4,128)S(1)} %get-tuple-element.190), channel_id=1, source_target_pairs={{0,8},{6,14},{13,21},{15,23},{20,28},{22,30},{27,35},{29,37},{34,4... | collective-permute-start | bytes 245768 | tf_op jit(solution)/shard_map/ppermute | solution.py:197
  68.6 6.1 %collective-permute-start.20 = (f32[8,5,4,128]{3,2,1,0:T(4,128)S(1)}, f32[8,5,4,128]{3,2,1,0:T(4,128)S(1)}, u32[]{:S(2)}, u32[]{:S(2)}) collective-permute-start(f32[8,5,4,128]{3,2,1,0:T(4,128)S(1)} %get-tuple-element.196), channel_id=1, source_target_pairs={{0,8},{2,10},{9,17},{15,23},{16,24},{22,30},{29,37},{31,39},{36,44... | collective-permute-start | bytes 245768 | tf_op jit(solution)/shard_map/ppermute | solution.py:197
  84.5 7.4 %collective-permute-start.32 = (f32[8,5,4,128]{3,2,1,0:T(4,128)S(1)}, f32[8,5,4,128]{3,2,1,0:T(4,128)S(1)}, u32[]{:S(2)}, u32[]{:S(2)}) collective-permute-start(f32[8,5,4,128]{3,2,1,0:T(4,128)S(1)} %get-tuple-element.214), channel_id=1, source_target_pairs={{0,8},{6,14},{13,21},{15,23},{20,28},{22,30},{27,35},{29,37},{34,4... | collective-permute-start | bytes 245768 | tf_op jit(solution)/shard_map/ppermute | solution.py:197
  96.0 8.2 %collective-permute-start.36 = (f32[8,5,4,128]{3,2,1,0:T(4,128)S(1)}, f32[8,5,4,128]{3,2,1,0:T(4,128)S(1)}, u32[]{:S(2)}, u32[]{:S(2)}) collective-permute-start(f32[8,5,4,128]{3,2,1,0:T(4,128)S(1)} %get-tuple-element.220), channel_id=1, source_target_pairs={{0,8},{2,10},{9,17},{15,23},{16,24},{22,30},{29,37},{31,39},{36,44... | collective-permute-start | bytes 245768 | tf_op jit(solution)/shard_map/ppermute | solution.py:197
  114.2 5.2 %early.1 = (f32[8192,128]{1,0:T(8,128)S(1)}, s32[128,128]{1,0:T(8,128)S(1)}) custom-call(f32[256,128]{1,0:T(8,128)S(1)} %bitcast.157, f32[8192,128]{1,0:T(8,128)S(1)} %late.1.picks_in.refs_6_), custom_call_target="tpu_custom_call", output_to_operand_aliasing={{0}: (1, {})} | custom-call | tf_op jit(solution)/shard_map/early/pallas_call | solution.py:254
  130.2 45.1 %collective-permute-done.58.refs_0_ = f32[8,5,4,128]{3,2,1,0:T(4,128)S(1)} collective-permute-done((f32[8,5,4,128]{3,2,1,0:T(4,128)S(1)}, f32[8,5,4,128]{3,2,1,0:T(4,128)S(1)}, u32[]{:S(2)}, u32[]{:S(2)}) %collective-permute-start.58) | collective-permute-done | bytes 81952 | tf_op jit(solution)/shard_map/ppermute | solution.py:197
  179.3 8.6 %collective-permute-done.62.refs_0_ = f32[8,5,4,128]{3,2,1,0:T(4,128)S(1)} collective-permute-done((f32[8,5,4,128]{3,2,1,0:T(4,128)S(1)}, f32[8,5,4,128]{3,2,1,0:T(4,128)S(1)}, u32[]{:S(2)}, u32[]{:S(2)}) %collective-permute-start.62) | collective-permute-done | bytes 81952 | tf_op jit(solution)/shard_map/ppermute | solution.py:197
  197.5 21.2 %collective-permute-done.74.refs_0_ = f32[8,5,4,128]{3,2,1,0:T(4,128)S(1)} collective-permute-done((f32[8,5,4,128]{3,2,1,0:T(4,128)S(1)}, f32[8,5,4,128]{3,2,1,0:T(4,128)S(1)}, u32[]{:S(2)}, u32[]{:S(2)}) %collective-permute-start.74) | collective-permute-done | bytes 81952 | tf_op jit(solution)/shard_map/ppermute | solution.py:197
  222.7 7.7 %collective-permute-done.78.refs_0_ = f32[8,5,4,128]{3,2,1,0:T(4,128)S(1)} collective-permute-done((f32[8,5,4,128]{3,2,1,0:T(4,128)S(1)}, f32[8,5,4,128]{3,2,1,0:T(4,128)S(1)}, u32[]{:S(2)}, u32[]{:S(2)}) %collective-permute-start.78) | collective-permute-done | bytes 81952 | tf_op jit(solution)/shard_map/ppermute | solution.py:197
  240.0 36.2 %collective-permute-done.90.refs_0_ = f32[8,5,4,128]{3,2,1,0:T(4,128)S(1)} collective-permute-done((f32[8,5,4,128]{3,2,1,0:T(4,128)S(1)}, f32[8,5,4,128]{3,2,1,0:T(4,128)S(1)}, u32[]{:S(2)}, u32[]{:S(2)}) %collective-permute-start.90) | collective-permute-done | bytes 81952 | tf_op jit(solution)/shard_map/ppermute | solution.py:197
  280.9 7.7 %collective-permute-done.94.refs_0_ = f32[8,5,4,128]{3,2,1,0:T(4,128)S(1)} collective-permute-done((f32[8,5,4,128]{3,2,1,0:T(4,128)S(1)}, f32[8,5,4,128]{3,2,1,0:T(4,128)S(1)}, u32[]{:S(2)}, u32[]{:S(2)}) %collective-permute-start.94) | collective-permute-done | bytes 81952 | tf_op jit(solution)/shard_map/ppermute | solution.py:197
  288.7 1.3 backward.49
  290.0 13.8 %serve.1 = f32[256,128]{1,0:T(8,128)} custom-call(s32[128,128]{1,0:T(8,128)S(1)} %get-tuple-element.161.refs_6_.index, f32[8192,128]{1,0:T(8,128)S(1)} %get-tuple-element.162.picks, f32[4096,128]{1,0:T(8,128)S(1)} %get-tuple-element.311.swept.swept_in), custom_call_target="tpu_custom_call" | custom-call | tf_op jit(solution)/shard_map/serve/pallas_call | solution.py:292
  303.8 45.8 %all-to-all-start.1 = ((f32[256,1,128]{2,1,0:T(1,128)}), f32[256,1,128]{2,1,0:T(1,128)S(1)}, u32[]{:S(2)}, u32[]{:S(2)}) async-start(f32[256,1,128]{2,1,0:T(1,128)} %bitcast.18), calls=%async_computation.1 | async-start | bytes 262144 | tf_op jit(solution)/shard_map/all_to_all | solution.py:345
  349.7 12.9 %all-to-all-done.1 = f32[256,1,128]{2,1,0:T(1,128)S(1)} async-done(((f32[256,1,128]{2,1,0:T(1,128)}), f32[256,1,128]{2,1,0:T(1,128)S(1)}, u32[]{:S(2)}, u32[]{:S(2)}) %all-to-all-start.1) | async-done | bytes 131104 | tf_op jit(solution)/shard_map/all_to_all | solution.py:345
  362.6 1.6 copy-done.4
  364.2 5.2 %finish.1 = (f32[8,5,8,1024]{3,2,1,0:T(8,128)}, f32[4096,128]{1,0:T(8,128)S(1)}) custom-call(s32[512]{0:T(512)S(1)} %bitcast.161, s32[512]{0:T(512)S(1)} %get-tuple-element.159.slots, f32[16384]{0:T(1024)S(1)} %dynamic_slice.3.values, f32[4096,128]{1,0:T(8,128)S(1)} %copy-done.4), custom_call_target="tpu_custom_call", output_to_operand_aliasing={{1}: (3, {})} | custom-call | tf_op jit(solution)/shard_map/finish/pallas_call | solution.py:331
  (260 shorter events, 87.7 us)
Async XLA Ops:
  9.0 4.7 %collective-permute-start = (f32[8,5,4,128]{3,2,1,0:T(4,128)S(1)}, f32[8,5,4,128]{3,2,1,0:T(4,128)S(1)}, u32[]{:S(2)}, u32[]{:S(2)}) collective-permute-start(f32[8,5,4,128]{3,2,1,0:T(4,128)S(1)} %get-tuple-element.166), channel_id=1, source_target_pairs={{0,8},{6,14},{13,21},{15,23},{20,28},{22,30},{27,35},{29,37},{34,4... | collective-permute-start | bytes 245768 | tf_op jit(solution)/shard_map/ppermute | solution.py:197
  15.0 20.1 %collective-permute-start.2 = (f32[8,5,4,128]{3,2,1,0:T(4,128)S(1)}, f32[8,5,4,128]{3,2,1,0:T(4,128)S(1)}, u32[]{:S(2)}, u32[]{:S(2)}) collective-permute-start(f32[8,5,4,128]{3,2,1,0:T(4,128)S(1)} %get-tuple-element.169), channel_id=1, source_target_pairs={{1,9},{7,15},{8,16},{14,22},{21,29},{23,31},{28,36},{30,38},{35,43... | collective-permute-start | bytes 245768 | tf_op jit(solution)/shard_map/ppermute | solution.py:197
  15.7 19.5 %collective-permute-start.3 = (f32[8,5,4,128]{3,2,1,0:T(4,128)S(1)}, f32[8,5,4,128]{3,2,1,0:T(4,128)S(1)}, u32[]{:S(2)}, u32[]{:S(2)}) collective-permute-start(f32[8,5,4,128]{3,2,1,0:T(4,128)S(1)} %get-tuple-element.170), channel_id=1, source_target_pairs={{1,2},{8,9},{14,15},{21,22},{28,29},{30,31},{35,36},{37,38},{42,43... | collective-permute-start | bytes 245768 | tf_op jit(solution)/shard_map/ppermute | solution.py:197
  16.3 31.8 %all-to-all-start = ((f32[256,1,128]{2,1,0:T(1,128)}), f32[256,1,128]{2,1,0:T(1,128)S(1)}, u32[]{:S(2)}, u32[]{:S(2)}) async-start(f32[256,1,128]{2,1,0:T(1,128)} %bitcast.12), calls=%async_computation | async-start | bytes 262144 | tf_op jit(solution)/shard_map/all_to_all | solution.py:345
  40.0 4.1 %collective-permute-start.4 = (f32[8,5,4,128]{3,2,1,0:T(4,128)S(1)}, f32[8,5,4,128]{3,2,1,0:T(4,128)S(1)}, u32[]{:S(2)}, u32[]{:S(2)}) collective-permute-start(f32[8,5,4,128]{3,2,1,0:T(4,128)S(1)} %get-tuple-element.172), channel_id=1, source_target_pairs={{0,8},{2,10},{9,17},{15,23},{16,24},{22,30},{29,37},{31,39},{36,44... | collective-permute-start | bytes 245768 | tf_op jit(solution)/shard_map/ppermute | solution.py:197
  56.5 9.4 %collective-permute-start.16 = (f32[8,5,4,128]{3,2,1,0:T(4,128)S(1)}, f32[8,5,4,128]{3,2,1,0:T(4,128)S(1)}, u32[]{:S(2)}, u32[]{:S(2)}) collective-permute-start(f32[8,5,4,128]{3,2,1,0:T(4,128)S(1)} %get-tuple-element.190), channel_id=1, source_target_pairs={{0,8},{6,14},{13,21},{15,23},{20,28},{22,30},{27,35},{29,37},{34,4... | collective-permute-start | bytes 245768 | tf_op jit(solution)/shard_map/ppermute | solution.py:197
  68.6 7.6 %collective-permute-start.20 = (f32[8,5,4,128]{3,2,1,0:T(4,128)S(1)}, f32[8,5,4,128]{3,2,1,0:T(4,128)S(1)}, u32[]{:S(2)}, u32[]{:S(2)}) collective-permute-start(f32[8,5,4,128]{3,2,1,0:T(4,128)S(1)} %get-tuple-element.196), channel_id=1, source_target_pairs={{0,8},{2,10},{9,17},{15,23},{16,24},{22,30},{29,37},{31,39},{36,44... | collective-permute-start | bytes 245768 | tf_op jit(solution)/shard_map/ppermute | solution.py:197
  84.5 8.8 %collective-permute-start.32 = (f32[8,5,4,128]{3,2,1,0:T(4,128)S(1)}, f32[8,5,4,128]{3,2,1,0:T(4,128)S(1)}, u32[]{:S(2)}, u32[]{:S(2)}) collective-permute-start(f32[8,5,4,128]{3,2,1,0:T(4,128)S(1)} %get-tuple-element.214), channel_id=1, source_target_pairs={{0,8},{6,14},{13,21},{15,23},{20,28},{22,30},{27,35},{29,37},{34,4... | collective-permute-start | bytes 245768 | tf_op jit(solution)/shard_map/ppermute | solution.py:197
  96.0 9.7 %collective-permute-start.36 = (f32[8,5,4,128]{3,2,1,0:T(4,128)S(1)}, f32[8,5,4,128]{3,2,1,0:T(4,128)S(1)}, u32[]{:S(2)}, u32[]{:S(2)}) collective-permute-start(f32[8,5,4,128]{3,2,1,0:T(4,128)S(1)} %get-tuple-element.220), channel_id=1, source_target_pairs={{0,8},{2,10},{9,17},{15,23},{16,24},{22,30},{29,37},{31,39},{36,44... | collective-permute-start | bytes 245768 | tf_op jit(solution)/shard_map/ppermute | solution.py:197
  112.6 6.9 %collective-permute-start.46 = (f32[8,5,4,128]{3,2,1,0:T(4,128)S(1)}, f32[8,5,4,128]{3,2,1,0:T(4,128)S(1)}, u32[]{:S(2)}, u32[]{:S(2)}) collective-permute-start(f32[8,5,4,128]{3,2,1,0:T(4,128)S(1)} %get-tuple-element.235), channel_id=1, source_target_pairs={{5,13},{7,15},{12,20},{14,22},{19,27},{21,29},{26,34},{28,36},{33,... | collective-permute-start | bytes 245768 | tf_op jit(solution)/shard_map/ppermute | solution.py:197
  113.4 6.1 %collective-permute-start.47 = (f32[8,5,4,128]{3,2,1,0:T(4,128)S(1)}, f32[8,5,4,128]{3,2,1,0:T(4,128)S(1)}, u32[]{:S(2)}, u32[]{:S(2)}) collective-permute-start(f32[8,5,4,128]{3,2,1,0:T(4,128)S(1)} %get-tuple-element.236), channel_id=1, source_target_pairs={{5,6},{12,13},{14,15},{19,20},{21,22},{26,27},{28,29},{33,34},{35,... | collective-permute-start | bytes 245768 | tf_op jit(solution)/shard_map/ppermute | solution.py:197
  127.6 47.7 %collective-permute-start.58 = (f32[8,5,4,128]{3,2,1,0:T(4,128)S(1)}, f32[8,5,4,128]{3,2,1,0:T(4,128)S(1)}, u32[]{:S(2)}, u32[]{:S(2)}) collective-permute-start(f32[8,5,4,128]{3,2,1,0:T(4,128)S(1)} %get-tuple-element.254), channel_id=1, source_target_pairs={{8,0},{10,2},{17,9},{23,15},{24,16},{30,22},{37,29},{39,31},{44,36... | collective-permute-start | bytes 245768 | tf_op jit(solution)/shard_map/ppermute | solution.py:197
  128.9 46.4 %collective-permute-start.59 = (f32[8,5,4,128]{3,2,1,0:T(4,128)S(1)}, f32[8,5,4,128]{3,2,1,0:T(4,128)S(1)}, u32[]{:S(2)}, u32[]{:S(2)}) collective-permute-start(f32[8,5,4,128]{3,2,1,0:T(4,128)S(1)} %get-tuple-element.255), channel_id=1, source_target_pairs={{1,0},{3,2},{10,9},{17,16},{23,22},{30,29},{37,36},{39,38},{44,43}... | collective-permute-start | bytes 245768 | tf_op jit(solution)/shard_map/ppermute | solution.py:197
  176.7 11.2 %collective-permute-start.62 = (f32[8,5,4,128]{3,2,1,0:T(4,128)S(1)}, f32[8,5,4,128]{3,2,1,0:T(4,128)S(1)}, u32[]{:S(2)}, u32[]{:S(2)}) collective-permute-start(f32[8,5,4,128]{3,2,1,0:T(4,128)S(1)} %get-tuple-element.260), channel_id=1, source_target_pairs={{8,0},{14,6},{21,13},{23,15},{28,20},{30,22},{35,27},{37,29},{42,3... | collective-permute-start | bytes 245768 | tf_op jit(solution)/shard_map/ppermute | solution.py:197
  178.0 9.9 %collective-permute-start.63 = (f32[8,5,4,128]{3,2,1,0:T(4,128)S(1)}, f32[8,5,4,128]{3,2,1,0:T(4,128)S(1)}, u32[]{:S(2)}, u32[]{:S(2)}) collective-permute-start(f32[8,5,4,128]{3,2,1,0:T(4,128)S(1)} %get-tuple-element.261), channel_id=1, source_target_pairs={{1,0},{7,6},{14,13},{21,20},{23,22},{28,27},{30,29},{35,34},{37,36... | collective-permute-start | bytes 245768 | tf_op jit(solution)/shard_map/ppermute | solution.py:197
  194.9 23.8 %collective-permute-start.74 = (f32[8,5,4,128]{3,2,1,0:T(4,128)S(1)}, f32[8,5,4,128]{3,2,1,0:T(4,128)S(1)}, u32[]{:S(2)}, u32[]{:S(2)}) collective-permute-start(f32[8,5,4,128]{3,2,1,0:T(4,128)S(1)} %get-tuple-element.278), channel_id=1, source_target_pairs={{8,0},{10,2},{17,9},{23,15},{24,16},{30,22},{37,29},{39,31},{44,36... | collective-permute-start | bytes 245768 | tf_op jit(solution)/shard_map/ppermute | solution.py:197
  196.2 22.5 %collective-permute-start.75 = (f32[8,5,4,128]{3,2,1,0:T(4,128)S(1)}, f32[8,5,4,128]{3,2,1,0:T(4,128)S(1)}, u32[]{:S(2)}, u32[]{:S(2)}) collective-permute-start(f32[8,5,4,128]{3,2,1,0:T(4,128)S(1)} %get-tuple-element.279), channel_id=1, source_target_pairs={{1,0},{3,2},{10,9},{17,16},{23,22},{30,29},{37,36},{39,38},{44,43}... | collective-permute-start | bytes 245768 | tf_op jit(solution)/shard_map/ppermute | solution.py:197
  220.1 10.3 %collective-permute-start.78 = (f32[8,5,4,128]{3,2,1,0:T(4,128)S(1)}, f32[8,5,4,128]{3,2,1,0:T(4,128)S(1)}, u32[]{:S(2)}, u32[]{:S(2)}) collective-permute-start(f32[8,5,4,128]{3,2,1,0:T(4,128)S(1)} %get-tuple-element.284), channel_id=1, source_target_pairs={{8,0},{14,6},{21,13},{23,15},{28,20},{30,22},{35,27},{37,29},{42,3... | collective-permute-start | bytes 245768 | tf_op jit(solution)/shard_map/ppermute | solution.py:197
  221.4 9.1 %collective-permute-start.79 = (f32[8,5,4,128]{3,2,1,0:T(4,128)S(1)}, f32[8,5,4,128]{3,2,1,0:T(4,128)S(1)}, u32[]{:S(2)}, u32[]{:S(2)}) collective-permute-start(f32[8,5,4,128]{3,2,1,0:T(4,128)S(1)} %get-tuple-element.285), channel_id=1, source_target_pairs={{1,0},{7,6},{14,13},{21,20},{23,22},{28,27},{30,29},{35,34},{37,36... | collective-permute-start | bytes 245768 | tf_op jit(solution)/shard_map/ppermute | solution.py:197
  237.4 38.8 %collective-permute-start.90 = (f32[8,5,4,128]{3,2,1,0:T(4,128)S(1)}, f32[8,5,4,128]{3,2,1,0:T(4,128)S(1)}, u32[]{:S(2)}, u32[]{:S(2)}) collective-permute-start(f32[8,5,4,128]{3,2,1,0:T(4,128)S(1)} %get-tuple-element.302), channel_id=1, source_target_pairs={{8,0},{10,2},{17,9},{23,15},{24,16},{30,22},{37,29},{39,31},{44,36... | collective-permute-start | bytes 245768 | tf_op jit(solution)/shard_map/ppermute | solution.py:197
  238.7 37.5 %collective-permute-start.91 = (f32[8,5,4,128]{3,2,1,0:T(4,128)S(1)}, f32[8,5,4,128]{3,2,1,0:T(4,128)S(1)}, u32[]{:S(2)}, u32[]{:S(2)}) collective-permute-start(f32[8,5,4,128]{3,2,1,0:T(4,128)S(1)} %get-tuple-element.303), channel_id=1, source_target_pairs={{1,0},{3,2},{10,9},{17,16},{23,22},{30,29},{37,36},{39,38},{44,43}... | collective-permute-start | bytes 245768 | tf_op jit(solution)/shard_map/ppermute | solution.py:197
  278.3 10.3 %collective-permute-start.94 = (f32[8,5,4,128]{3,2,1,0:T(4,128)S(1)}, f32[8,5,4,128]{3,2,1,0:T(4,128)S(1)}, u32[]{:S(2)}, u32[]{:S(2)}) collective-permute-start(f32[8,5,4,128]{3,2,1,0:T(4,128)S(1)} %get-tuple-element.308), channel_id=1, source_target_pairs={{8,0},{14,6},{21,13},{23,15},{28,20},{30,22},{35,27},{37,29},{42,3... | collective-permute-start | bytes 245768 | tf_op jit(solution)/shard_map/ppermute | solution.py:197
  279.6 9.0 %collective-permute-start.95 = (f32[8,5,4,128]{3,2,1,0:T(4,128)S(1)}, f32[8,5,4,128]{3,2,1,0:T(4,128)S(1)}, u32[]{:S(2)}, u32[]{:S(2)}) collective-permute-start(f32[8,5,4,128]{3,2,1,0:T(4,128)S(1)} %get-tuple-element.309), channel_id=1, source_target_pairs={{1,0},{7,6},{14,13},{21,20},{23,22},{28,27},{30,29},{35,34},{37,36... | collective-permute-start | bytes 245768 | tf_op jit(solution)/shard_map/ppermute | solution.py:197
  303.8 58.8 %all-to-all-start.1 = ((f32[256,1,128]{2,1,0:T(1,128)}), f32[256,1,128]{2,1,0:T(1,128)S(1)}, u32[]{:S(2)}, u32[]{:S(2)}) async-start(f32[256,1,128]{2,1,0:T(1,128)} %bitcast.18), calls=%async_computation.1 | async-start | bytes 262144 | tf_op jit(solution)/shard_map/all_to_all | solution.py:345
  (88 other events, 212.0 us)
